TPU v7x, 32 devices: a whole 2x2x4 slice. The times are simulated.
32 devices in a mesh: samples: 4 (over y, x), features: 4 (over z), rhs: 2 (over core).
Axes of the slice: x: 2, y: 2, z: 4, core: 2. Of those that a mesh axis runs over, the one named last changes fastest.
Arguments:
- design: bfloat16 [32768, 32768], P(('samples', 'rhs'), 'features'), may hold values from -0.03125 to 0.03125
- right_side: float32 [32768, 64], P('features', 'rhs'), may hold values from -6 to 6
- factor: bfloat16 [32768, 768], P('features', 'rhs'), may hold values from -0.03125 to 0.03125
- nystrom_values: float32 [768], replicated, may hold values from 0.5 to 3
Outputs:
- solution: float32 [32768, 64], P('features', 'rhs')
- residual: float32 [32768, 64], P('features', 'rhs')
All inputs are finite; a program needn't handle non-finite values.
Results may differ from a plain program's by a relative error of at most 0.0181.
Values may be sent and summed in bfloat16 or wider, within the bound.
A program may use at most 192 MiB of HBM per device.

v0:
```python
import jax
import jax.numpy as jnp
from jax import lax
from jax.sharding import PartitionSpec as P

ITERS = 3
ridge_weight = 1.0


def inner_prod(left, right):
    return lax.dot_general(
        left,
        right,
        (((0,), (0,)), ((), ())),
        precision=lax.Precision.HIGHEST,
        preferred_element_type=jnp.float32,
    )


def split_parts(values):
    upper = values.astype(jnp.bfloat16)
    widened = lax.optimization_barrier(upper).astype(jnp.float32)
    lower = (values - widened).astype(jnp.bfloat16)
    return (upper, lower)


def factor_inner(factor_narrow, values):
    upper, lower = split_parts(values)
    dims = (((0,), (0,)), ((), ()))
    first = lax.dot_general(factor_narrow, upper, dims, preferred_element_type=jnp.float32)
    second = lax.dot_general(factor_narrow, lower, dims, preferred_element_type=jnp.float32)
    return first + second


def factor_times(factor_narrow, values):
    upper, lower = split_parts(values)
    first = jnp.dot(factor_narrow, upper, preferred_element_type=jnp.float32)
    second = jnp.dot(factor_narrow, lower, preferred_element_type=jnp.float32)
    return first + second


def shards(design, right_side, factor, nystrom_values):
    feat_rows, col_share = right_side.shape
    shrink = (1.0 + jnp.min(nystrom_values)) / (1.0 + nystrom_values) - 1.0
    columns = lax.all_gather(right_side, "rhs", axis=1, tiled=True)
    residual = columns
    basis_rows = lax.all_gather(factor, "rhs", axis=1, tiled=True)

    def totals(values):
        return lax.psum(values, "features")

    def expand(projected):
        return factor_times(basis_rows, shrink[:, None] * projected)

    projected = totals(factor_inner(basis_rows, residual))
    direction = residual + expand(projected)
    solution = jnp.zeros_like(residual)
    for iteration in range(ITERS):
        narrow = direction.astype(jnp.bfloat16)
        apply_partial_value = jnp.dot(design, narrow, preferred_element_type=jnp.float32)
        narrow_images = lax.psum(apply_partial_value, "features").astype(jnp.bfloat16)
        feature_term = lax.dot_general(
            design, narrow_images, (((0,), (0,)), ((), ())), preferred_element_type=jnp.float32
        )
        summed = lax.psum(feature_term, ("samples", "rhs"))
        applied = summed + ridge_weight * direction
        gram_block, cross_term, image_res, image_image, factor_image = totals(
            (
                inner_prod(direction, applied),
                inner_prod(direction, residual),
                inner_prod(applied, residual),
                inner_prod(applied, applied),
                factor_inner(basis_rows, applied),
            )
        )
        gram_block = 0.5 * (gram_block + gram_block.T)
        chol_lower = jnp.linalg.cholesky(gram_block)
        unit_dir = jax.scipy.linalg.solve_triangular(chol_lower, direction.T, lower=True).T
        unit_img = jax.scipy.linalg.solve_triangular(chol_lower, applied.T, lower=True).T
        step_coef = jax.scipy.linalg.solve_triangular(chol_lower, cross_term, lower=True)
        solution = solution + jnp.dot(unit_dir, step_coef, precision=lax.Precision.HIGHEST)
        residual = residual - jnp.dot(unit_img, step_coef, precision=lax.Precision.HIGHEST)
        if iteration + 1 < ITERS:
            back_step = jax.scipy.linalg.solve_triangular(
                chol_lower, step_coef, lower=True, trans=1
            )
            projected = projected - jnp.dot(
                factor_image, back_step, precision=lax.Precision.HIGHEST
            )
            scaled = residual + expand(projected)
            image_new = image_res - jnp.dot(image_image, back_step, precision=lax.Precision.HIGHEST)
            image_new = image_new + inner_prod(factor_image, shrink[:, None] * projected)
            next_coef = -jax.scipy.linalg.solve_triangular(chol_lower, image_new, lower=True)
            direction = scaled + jnp.dot(unit_dir, next_coef, precision=lax.Precision.HIGHEST)
    column_start = lax.axis_index("rhs") * col_share
    out_sol = lax.dynamic_slice_in_dim(solution, column_start, col_share, 1)
    out_res = lax.dynamic_slice_in_dim(residual, column_start, col_share, 1)
    return (out_sol, out_res)


def solution(mesh):
    placed = (P(("samples", "rhs"), "features"), P("features", "rhs"), P("features", "rhs"), P())
    return jax.shard_map(
        shards,
        mesh=mesh,
        in_specs=placed,
        out_specs=(P("features", "rhs"), P("features", "rhs")),
        check_vma=False,
    )
```

profile of v0, /device:TPU:0, one launch (start us, length us, event | category | flops | bytes accessed | tf_op | source)
XLA Modules:
  0.0 853.2 jit_solution(9998928612973178029)
XLA Ops:
  10.0 12.9 %all-gather.3.cloned.1.call-done = f32[8192,64]{0,1:T(8,128)} async-done(((f32[8192,32]{0,1:T(8,128)}), f32[8192,64]{0,1:T(8,128)}) %all-gather.3.cloned.1.call-update) | async-done | bytes 2097168 | tf_op jit(solution)/shard_map/all_gather | solution.py:45
  24.7 25.6 %all-gather.5.cloned.1.call-done = bf16[8192,768]{1,0:T(8,128)(2,1)} async-done(((bf16[8192,384]{1,0:T(8,128)(2,1)}), bf16[8192,768]{1,0:T(8,128)(2,1)}) %all-gather.5.cloned.1.call-update) | async-done | bytes 12582928 | tf_op jit(solution)/shard_map/all_gather | solution.py:47
  50.3 7.0 convolution_bitcast_fusion.6
  61.5 36.2 %all-reduce.15.cloned.1.call-done = f32[768,64]{0,1:T(8,128)} async-done(((f32[768,64]{0,1:T(8,128)}), f32[768,64]{0,1:T(8,128)}) %all-reduce.15.cloned.1.call-update) | async-done | bytes 196624 | tf_op jit(solution)/shard_map/psum | solution.py:50
  98.7 8.5 fusion.67
  107.2 9.8 %fusion.3 = f32[8192,64]{0,1:T(8,128)} fusion(f32[8192,64]{0,1:T(8,128)S(1)} %copy-done.1, f32[64,8192]{1,0:T(8,128)S(1)} %fusion.67, bf16[8192,768]{1,0:T(8,128)(2,1)} %all-gather.5.cloned.1.call-done, bf16[768,64]{0,1:T(8,128)(2,1)S(1)} %multiply_convert_fusion, f32[768,64]{0,1:T(8,128)S(1)} %copy-done.19, f32[768]{0:T(1024)S(1)} %divide_add_fusion), kind=kOutput, calls=%fused_computation.13 | convolution fusion | flops 806551552 | bytes 19172352 | tf_op jit(solution)/shard_map/dot_general | solution.py:38
  117.1 30.4 %convolution_bitcast_fusion.5 = f32[4096,64]{0,1:T(8,128)S(1)} fusion(bf16[4096,8192]{1,0:T(8,128)(2,1)} %param.11, f32[8192,64]{0,1:T(8,128)} %fusion.3), kind=kOutput, calls=%fused_computation.18 | convolution fusion | flops 4295491584 | bytes 70254592 | tf_op jit(solution)/shard_map/dot_general | solution.py:60
  147.4 42.8 %all-reduce.30 = bf16[4096,64]{0,1:T(8,128)(2,1)} all-reduce(f32[4096,64]{0,1:T(8,128)S(1)} %convolution_bitcast_fusion.5), channel_id=1, replica_groups=mesh['samples'=4,'features'=4,'rhs'=2] {'features'}, use_global_device_ids=true, to_apply=%region_2.0 | all-reduce | flops 262144 | bytes 1572864 | tf_op jit(solution)/shard_map/psum | solution.py:61
  190.2 25.9 %convolution_bitcast_fusion.2 = f32[8192,64]{0,1:T(8,128)} fusion(bf16[4096,8192]{1,0:T(8,128)(2,1)} %param.11, bf16[4096,64]{0,1:T(8,128)(2,1)} %all-reduce.30), kind=kOutput, calls=%fused_computation.10 | convolution fusion | flops 4294967296 | bytes 69730304 | tf_op jit(solution)/shard_map/dot_general | solution.py:62
  220.2 57.3 %all-reduce.17.cloned.1.call-done = f32[8192,64]{0,1:T(8,128)} async-done(((f32[8192,64]{0,1:T(8,128)}), f32[8192,64]{0,1:T(8,128)}) %all-reduce.17.cloned.1.call-update) | async-done | bytes 2097168 | tf_op jit(solution)/shard_map/psum | solution.py:65
  287.3 6.8 fusion.71
  294.2 7.6 fusion.22
  302.0 19.4 %all-reduce.29.cloned.1.call-done = (f32[64,64]{1,0:T(8,128)}, f32[64,64]{1,0:T(8,128)}, f32[64,64]{1,0:T(8,128)}, f32[64,64]{1,0:T(8,128)}) async-done(((f32[64,64]{1,0:T(8,128)}, f32[64,64]{1,0:T(8,128)}, f32[64,64]{1,0:T(8,128)}, f32[64,64]{1,0:T(8,128)}), (f32[64,64]{1,0:T(8,128)}, f32[64,64]{1,0:T(8,128)}, f32[64,64]{1,0:T(8,128)}, f32[64,64]{1,0:T(8,128)})) %all-reduce.29.cloned.1.call-update) | async-done | bytes 65552 | tf_op jit(solution)/shard_map/psum | solution.py:50
  344.5 14.6 %all-reduce.19.cloned.1.call-done = f32[768,64]{0,1:T(8,128)} async-done(((f32[768,64]{0,1:T(8,128)}), f32[768,64]{0,1:T(8,128)}) %all-reduce.19.cloned.1.call-update) | async-done | bytes 196624 | tf_op jit(solution)/shard_map/psum | solution.py:50
  362.1 8.4 fusion.72
  370.6 8.6 %fusion.4 = f32[8192,64]{0,1:T(8,128)S(1)} fusion(f32[8192,64]{0,1:T(8,128)S(1)} %convolution_subtract_fusion.1, f32[64,8192]{1,0:T(8,128)S(1)} %fusion.72, bf16[8192,768]{1,0:T(8,128)(2,1)} %all-gather.5.cloned.1.call-done, bf16[768,64]{0,1:T(8,128)(2,1)S(1)} %get-tuple-element.20, f32[768,64]{0,1:T(8,128)S(1)} %get-tuple-element.21, ...), kind=kOutput, calls=%fused_computation.14 | convolution fusion | flops 806551552 | bytes 19172352 | tf_op jit(solution)/shard_map/dot_general | solution.py:38
  381.5 27.8 %convolution_bitcast_fusion.4 = f32[4096,64]{0,1:T(8,128)S(1)} fusion(bf16[4096,8192]{1,0:T(8,128)(2,1)} %param.11, f32[8192,64]{0,1:T(8,128)S(1)} %convolution_add_fusion.2), kind=kOutput, calls=%fused_computation.17 | convolution fusion | flops 4295491584 | bytes 70254592 | tf_op jit(solution)/shard_map/dot_general | solution.py:60
  409.4 42.1 %all-reduce.31 = bf16[4096,64]{0,1:T(8,128)(2,1)} all-reduce(f32[4096,64]{0,1:T(8,128)S(1)} %convolution_bitcast_fusion.4), channel_id=1, replica_groups=mesh['samples'=4,'features'=4,'rhs'=2] {'features'}, use_global_device_ids=true, to_apply=%region_11.0 | all-reduce | flops 262144 | bytes 1572864 | tf_op jit(solution)/shard_map/psum | solution.py:61
  451.5 25.9 %convolution_bitcast_fusion.1 = f32[8192,64]{0,1:T(8,128)} fusion(bf16[4096,8192]{1,0:T(8,128)(2,1)} %param.11, bf16[4096,64]{0,1:T(8,128)(2,1)} %all-reduce.31), kind=kOutput, calls=%fused_computation.5 | convolution fusion | flops 4294967296 | bytes 69730304 | tf_op jit(solution)/shard_map/dot_general | solution.py:62
  481.9 57.4 %all-reduce.21.cloned.1.call-done = f32[8192,64]{0,1:T(8,128)} async-done(((f32[8192,64]{0,1:T(8,128)}), f32[8192,64]{0,1:T(8,128)}) %all-reduce.21.cloned.1.call-update) | async-done | bytes 2097168 | tf_op jit(solution)/shard_map/psum | solution.py:65
  549.5 6.8 fusion.78
  556.4 7.6 fusion.23
  564.2 19.4 %all-reduce.27.cloned.1.call-done = (f32[64,64]{1,0:T(8,128)}, f32[64,64]{1,0:T(8,128)}, f32[64,64]{1,0:T(8,128)}, f32[64,64]{1,0:T(8,128)}) async-done(((f32[64,64]{1,0:T(8,128)}, f32[64,64]{1,0:T(8,128)}, f32[64,64]{1,0:T(8,128)}, f32[64,64]{1,0:T(8,128)}), (f32[64,64]{1,0:T(8,128)}, f32[64,64]{1,0:T(8,128)}, f32[64,64]{1,0:T(8,128)}, f32[64,64]{1,0:T(8,128)})) %all-reduce.27.cloned.1.call-update) | async-done | bytes 65552 | tf_op jit(solution)/shard_map/psum | solution.py:50
  585.3 5.8 cholesky.70
  606.6 14.8 %all-reduce.23.cloned.1.call-done = f32[768,64]{0,1:T(8,128)} async-done(((f32[768,64]{0,1:T(8,128)}), f32[768,64]{0,1:T(8,128)}) %all-reduce.23.cloned.1.call-update) | async-done | bytes 196624 | tf_op jit(solution)/shard_map/psum | solution.py:50
  624.5 8.4 fusion.79
  632.9 8.6 %fusion.5 = f32[8192,64]{0,1:T(8,128)S(1)} fusion(f32[8192,64]{0,1:T(8,128)S(1)} %convolution_subtract_fusion, f32[64,8192]{1,0:T(8,128)S(1)} %fusion.79, bf16[8192,768]{1,0:T(8,128)(2,1)} %all-gather.5.cloned.1.call-done, f32[768,64]{0,1:T(8,128)S(1)} %get-tuple-element.23, bf16[768,64]{0,1:T(8,128)(2,1)S(1)} %get-tuple-element.22), kind=kOutput, calls=%fused_computation.15 | convolution fusion | flops 806502400 | bytes 19169280 | tf_op jit(solution)/shard_map/dot_general | solution.py:38
  644.0 27.1 %convolution_bitcast_fusion.3 = f32[4096,64]{0,1:T(8,128)S(1)} fusion(bf16[4096,8192]{1,0:T(8,128)(2,1)} %param.11, f32[8192,64]{0,1:T(8,128)S(1)} %convolution_add_fusion), kind=kOutput, calls=%fused_computation.16 | convolution fusion | flops 4295491584 | bytes 70254592 | tf_op jit(solution)/shard_map/dot_general | solution.py:60
  671.1 42.1 %all-reduce.32 = bf16[4096,64]{0,1:T(8,128)(2,1)} all-reduce(f32[4096,64]{0,1:T(8,128)S(1)} %convolution_bitcast_fusion.3), channel_id=1, replica_groups=mesh['samples'=4,'features'=4,'rhs'=2] {'features'}, use_global_device_ids=true, to_apply=%region_18.0 | all-reduce | flops 262144 | bytes 1572864 | tf_op jit(solution)/shard_map/psum | solution.py:61
  713.2 25.9 %convolution_bitcast_fusion = f32[8192,64]{0,1:T(8,128)} fusion(bf16[4096,8192]{1,0:T(8,128)(2,1)} %param.11, bf16[4096,64]{0,1:T(8,128)(2,1)} %all-reduce.32), kind=kOutput, calls=%fused_computation | convolution fusion | flops 4294967296 | bytes 69730304 | tf_op jit(solution)/shard_map/dot_general | solution.py:62
  750.0 50.6 %all-reduce.25.cloned.1.call-done = f32[8192,64]{0,1:T(8,128)} async-done(((f32[8192,64]{0,1:T(8,128)}), f32[8192,64]{0,1:T(8,128)}) %all-reduce.25.cloned.1.call-update) | async-done | bytes 2097168 | tf_op jit(solution)/shard_map/psum | solution.py:65
  804.1 19.8 %all-reduce = (f32[64,64]{1,0:T(8,128)S(1)}, f32[64,64]{1,0:T(8,128)S(1)}) all-reduce(f32[64,64]{1,0:T(8,128)S(1)} %fusion.19, f32[64,64]{1,0:T(8,128)S(1)} %fusion.83), channel_id=1, replica_groups=mesh['samples'=4,'features'=4,'rhs'=2] {'features'}, use_global_device_ids=true, to_apply=%region_20.25 | all-reduce | flops 8192 | bytes 65536 | tf_op jit(solution)/shard_map/psum | solution.py:50
  (149 shorter events, 125.3 us)
Async XLA Ops:
  7.2 15.7 %all-gather.3.cloned.1.call-start = ((), (), s32[]{:S(2)}) async-start(), calls=%async_computation | async-start | bytes 3145728 | tf_op jit(solution)/shard_map/all_gather | solution.py:45
  7.9 42.4 %all-gather.5.cloned.1.call-start = ((), (), s32[]{:S(2)}) async-start(), calls=%async_computation.1 | async-start | bytes 18874368 | tf_op jit(solution)/shard_map/all_gather | solution.py:47
  8.7 89.1 %all-reduce.15.cloned.1.call-start = ((), (), s32[]{:S(2)}) async-start(), calls=%async_computation.2 | async-start | bytes 393216 | tf_op jit(solution)/shard_map/psum | solution.py:50
  22.8 27.4 %copy-start.1 = (f32[8192,64]{0,1:T(8,128)S(1)}, f32[8192,64]{0,1:T(8,128)}, u32[]{:S(2)}) copy-start(f32[8192,64]{0,1:T(8,128)} %all-gather.3.cloned.1.call-done) | copy-start | bytes 6291460
  50.3 8.2 copy-start
  61.5 216.0 %all-reduce.17.cloned.1.call-start = ((), (), s32[]{:S(2)}) async-start(), calls=%async_computation.3 | async-start | bytes 4194304 | tf_op jit(solution)/shard_map/psum | solution.py:65
  98.7 8.5 copy-start.19
  216.2 105.3 %all-reduce.29.cloned.1.call-start = ((), (), s32[]{:S(2)}) async-start(), calls=%async_computation.9 | async-start | bytes 262144 | tf_op jit(solution)/shard_map/psum | solution.py:50
  280.0 2.4 copy-start.4
  282.4 2.4 copy-start.2
  287.3 71.8 %all-reduce.19.cloned.1.call-start = ((), (), s32[]{:S(2)}) async-start(), calls=%async_computation.4 | async-start | bytes 393216 | tf_op jit(solution)/shard_map/psum | solution.py:50
  301.8 237.5 %all-reduce.21.cloned.1.call-start = ((), (), s32[]{:S(2)}) async-start(), calls=%async_computation.5 | async-start | bytes 4194304 | tf_op jit(solution)/shard_map/psum | solution.py:65
  340.0 2.2 copy-start.3
  342.2 19.4 %copy-start.24 = (f32[64,64]{1,0:T(8,128)S(1)}, f32[64,64]{1,0:T(8,128)}, u32[]{:S(2)}) copy-start(f32[64,64]{1,0:T(8,128)} %get-tuple-element.14) | copy-start | bytes 49156
  342.2 19.4 %copy-start.25 = (f32[64,64]{1,0:T(8,128)S(1)}, f32[64,64]{1,0:T(8,128)}, u32[]{:S(2)}) copy-start(f32[64,64]{1,0:T(8,128)} %get-tuple-element.15) | copy-start | bytes 49156
  344.3 26.2 %copy-start.7 = (f32[8192,64]{0,1:T(8,128)}, f32[8192,64]{0,1:T(8,128)S(1)}, u32[]{:S(2)}) copy-start(f32[8192,64]{0,1:T(8,128)S(1)} %convolution_subtract_fusion.1) | copy-start | bytes 6291460
  370.5 8.7 %copy-start.13 = (f32[64,8192]{1,0:T(8,128)S(1)}, f32[64,8192]{1,0:T(8,128)}, u32[]{:S(2)}) copy-start(f32[64,8192]{1,0:T(8,128)} %fusion.16) | copy-start | bytes 6291460
  381.5 96.4 %copy-start.5 = (f32[8192,64]{0,1:T(8,128)}, f32[8192,64]{0,1:T(8,128)S(1)}, u32[]{:S(2)}) copy-start(f32[8192,64]{0,1:T(8,128)S(1)} %convolution_add_fusion.2) | copy-start | bytes 6291460
  477.5 106.1 %all-reduce.27.cloned.1.call-start = ((), (), s32[]{:S(2)}) async-start(), calls=%async_computation.8 | async-start | bytes 262144 | tf_op jit(solution)/shard_map/psum | solution.py:50
  539.3 2.9 copy-start.8
  544.6 2.4 copy-start.6
  549.5 72.0 %all-reduce.23.cloned.1.call-start = ((), (), s32[]{:S(2)}) async-start(), calls=%async_computation.6 | async-start | bytes 393216 | tf_op jit(solution)/shard_map/psum | solution.py:50
  564.0 236.7 %all-reduce.25.cloned.1.call-start = ((), (), s32[]{:S(2)}) async-start(), calls=%async_computation.7 | async-start | bytes 4194304 | tf_op jit(solution)/shard_map/psum | solution.py:65
  602.2 2.2 copy-start.9
  604.4 19.7 %copy-start.22 = (f32[64,64]{1,0:T(8,128)S(1)}, f32[64,64]{1,0:T(8,128)}, u32[]{:S(2)}) copy-start(f32[64,64]{1,0:T(8,128)} %get-tuple-element.10) | copy-start | bytes 49156
  604.4 19.7 %copy-start.23 = (f32[64,64]{1,0:T(8,128)S(1)}, f32[64,64]{1,0:T(8,128)}, u32[]{:S(2)}) copy-start(f32[64,64]{1,0:T(8,128)} %get-tuple-element.11) | copy-start | bytes 49156
  606.5 26.5 %copy-start.10 = (f32[8192,64]{0,1:T(8,128)}, f32[8192,64]{0,1:T(8,128)S(1)}, u32[]{:S(2)}) copy-start(f32[8192,64]{0,1:T(8,128)S(1)} %convolution_subtract_fusion) | copy-start | bytes 6291460
  632.9 8.6 %copy-start.14 = (f32[64,8192]{1,0:T(8,128)S(1)}, f32[64,8192]{1,0:T(8,128)}, u32[]{:S(2)}) copy-start(f32[64,8192]{1,0:T(8,128)} %fusion.12) | copy-start | bytes 6291460
  739.9 5.0 copy-start.15
  744.9 3.3 copy-start.11
  840.4 4.1 copy-start.18
  842.4 2.2 copy-start.17
  (7 other events, 11.6 us)
Sparse Core Ops, SparseCore 0:
  9.5 13.2 all-gather.2
  24.4 25.8 all-gather.4
  61.6 36.1 all-reduce.14
  216.3 61.1 all-reduce.16
  287.4 33.9 all-reduce.28
  324.2 34.8 all-reduce.18
  477.6 61.6 all-reduce.20
  549.6 33.9 all-reduce.26
  586.5 34.9 all-reduce.22
  739.3 61.3 all-reduce.24
where the time goes:
time: 862 us; the launch traced here: 853 us
  matrix products  328 us (38%)
  waiting for transfers between devices  310 us (36%)
  blocking collectives  147 us (17%)
  other arithmetic  47.9 us (6%)
  between operations  15.6 us (2%)
    psum x3, waiting for transfers between devices, shards(): summed = lax.psum(feature_term, ('samples', 'rhs'))  165 us
    psum x3, blocking collectives, shards(): lax.psum(apply_partial_value, 'features').astype(jnp.bfloat16)  127 us
    psum x5, waiting for transfers between devices, totals(): return lax.psum(values, 'features')  105 us
    dot_general x3, matrix products, shards(): jnp.dot(design, narrow, preferred_element_type=jnp.float32)  85.3 us
    dot_general x3, matrix products, shards(): lax.dot_general(design, narrow_images, (((0,), (0,)), ((), ())), preferre...  77.8 us
    dot_general x12, matrix products, inner_prod(): lax.dot_general(left, right, (((0,), (0,)), ((), ())), precision=lax.Prec...  30.3 us
    dot_general x3, matrix products, factor_times(): second = jnp.dot(factor_narrow, lower, preferred_element_type=jnp.float32)  27.1 us
    all_gather x1, waiting for transfers between devices, shards(): basis_rows = lax.all_gather(factor, 'rhs', axis=1, tiled=True)  25.6 us
  transfers between devices with their start and end apart: 10, of which 10 were waited for; matrix products, arithmetic and copies ran while one was open for 11% of the time, Pallas kernels for 0%

commit v1 on v0

--- a/solution.py
+++ b/solution.py
@@ -62,7 +62,7 @@
         feature_term = lax.dot_general(
             design, narrow_images, (((0,), (0,)), ((), ())), preferred_element_type=jnp.float32
         )
-        summed = lax.psum(feature_term, ("samples", "rhs"))
+        summed = lax.psum(lax.psum(feature_term, "rhs"), "samples")
         applied = summed + ridge_weight * direction
         gram_block, cross_term, image_res, image_image, factor_image = totals(
             (

time: 862 us -> 963 us (1.12)
  waiting for transfers between devices: 310 us -> 411 us
    psum x3 -> x6, waiting for transfers between devices: 165 us -> 265 us  [shards(): summed = lax.psum(lax.psum(feature_term, 'rhs'), 'samples')]
  transfers between devices with their start and end apart: 10 -> 13, of which waited for: 10 -> 13; matrix products, arithmetic and copies ran while one was open for 11% -> 10% of each run, Pallas kernels for 0% -> 0%
where the time goes in v1:
time: 963 us; the launch traced here: 954 us
  waiting for transfers between devices  411 us (43%)
  matrix products  328 us (34%)
  blocking collectives  147 us (15%)
  other arithmetic  47.9 us (5%)
  between operations  15.4 us (2%)
    psum x6, waiting for transfers between devices, shards(): summed = lax.psum(lax.psum(feature_term, 'rhs'), 'samples')  265 us
    psum x3, blocking collectives, shards(): lax.psum(apply_partial_value, 'features').astype(jnp.bfloat16)  127 us
    psum x5, waiting for transfers between devices, totals(): return lax.psum(values, 'features')  107 us
    dot_general x3, matrix products, shards(): jnp.dot(design, narrow, preferred_element_type=jnp.float32)  85.3 us
    dot_general x3, matrix products, shards(): lax.dot_general(design, narrow_images, (((0,), (0,)), ((), ())), preferre...  77.8 us
    dot_general x12, matrix products, inner_prod(): lax.dot_general(left, right, (((0,), (0,)), ((), ())), precision=lax.Prec...  30.3 us
    dot_general x3, matrix products, factor_times(): second = jnp.dot(factor_narrow, lower, preferred_element_type=jnp.float32)  27.1 us
    all_gather x1, waiting for transfers between devices, shards(): basis_rows = lax.all_gather(factor, 'rhs', axis=1, tiled=True)  25.6 us
  transfers between devices with their start and end apart: 13, of which 13 were waited for; matrix products, arithmetic and copies ran while one was open for 10% of the time, Pallas kernels for 0%

profile of v1, /device:TPU:0, one launch (start us, length us, event | category | flops | bytes accessed | tf_op | source)
XLA Modules:
  0.0 954.5 jit_solution(14918473197212958825)
XLA Ops:
  10.0 12.9 %all-gather.3.cloned.1.call-done = f32[8192,64]{0,1:T(8,128)} async-done(((f32[8192,32]{0,1:T(8,128)}), f32[8192,64]{0,1:T(8,128)}) %all-gather.3.cloned.1.call-update) | async-done | bytes 2097168 | tf_op jit(solution)/shard_map/all_gather | solution.py:45
  24.7 25.6 %all-gather.5.cloned.1.call-done = bf16[8192,768]{1,0:T(8,128)(2,1)} async-done(((bf16[8192,384]{1,0:T(8,128)(2,1)}), bf16[8192,768]{1,0:T(8,128)(2,1)}) %all-gather.5.cloned.1.call-update) | async-done | bytes 12582928 | tf_op jit(solution)/shard_map/all_gather | solution.py:47
  50.3 7.0 convolution_bitcast_fusion.6
  61.5 36.2 %all-reduce.18.cloned.1.call-done = f32[768,64]{0,1:T(8,128)} async-done(((f32[768,64]{0,1:T(8,128)}), f32[768,64]{0,1:T(8,128)}) %all-reduce.18.cloned.1.call-update) | async-done | bytes 196624 | tf_op jit(solution)/shard_map/psum | solution.py:50
  98.7 8.5 fusion.67
  107.2 9.8 %fusion.3 = f32[8192,64]{0,1:T(8,128)} fusion(f32[8192,64]{0,1:T(8,128)S(1)} %copy-done.1, f32[64,8192]{1,0:T(8,128)S(1)} %fusion.67, bf16[8192,768]{1,0:T(8,128)(2,1)} %all-gather.5.cloned.1.call-done, bf16[768,64]{0,1:T(8,128)(2,1)S(1)} %multiply_convert_fusion, f32[768,64]{0,1:T(8,128)S(1)} %copy-done.19, f32[768]{0:T(1024)S(1)} %divide_add_fusion), kind=kOutput, calls=%fused_computation.13 | convolution fusion | flops 806551552 | bytes 19172352 | tf_op jit(solution)/shard_map/dot_general | solution.py:38
  117.1 30.4 %convolution_bitcast_fusion.5 = f32[4096,64]{0,1:T(8,128)S(1)} fusion(bf16[4096,8192]{1,0:T(8,128)(2,1)} %param.11, f32[8192,64]{0,1:T(8,128)} %fusion.3), kind=kOutput, calls=%fused_computation.18 | convolution fusion | flops 4295491584 | bytes 70254592 | tf_op jit(solution)/shard_map/dot_general | solution.py:60
  147.4 42.8 %all-reduce.39 = bf16[4096,64]{0,1:T(8,128)(2,1)} all-reduce(f32[4096,64]{0,1:T(8,128)S(1)} %convolution_bitcast_fusion.5), channel_id=1, replica_groups=mesh['samples'=4,'features'=4,'rhs'=2] {'features'}, use_global_device_ids=true, to_apply=%region_2.0 | all-reduce | flops 262144 | bytes 1572864 | tf_op jit(solution)/shard_map/psum | solution.py:61
  190.2 25.9 %convolution_bitcast_fusion.2 = f32[8192,64]{0,1:T(8,128)} fusion(bf16[4096,8192]{1,0:T(8,128)(2,1)} %param.11, bf16[4096,64]{0,1:T(8,128)(2,1)} %all-reduce.39), kind=kOutput, calls=%fused_computation.10 | convolution fusion | flops 4294967296 | bytes 69730304 | tf_op jit(solution)/shard_map/dot_general | solution.py:62
  216.2 20.8 %all-reduce.20.cloned.1.call-done = f32[8192,64]{0,1:T(8,128)} async-done(((f32[8192,64]{0,1:T(8,128)}), f32[8192,64]{0,1:T(8,128)}) %all-reduce.20.cloned.1.call-update) | async-done | bytes 2097168 | tf_op jit(solution)/shard_map/psum | solution.py:65
  241.1 69.6 %all-reduce.22.cloned.1.call-done = f32[8192,64]{0,1:T(8,128)} async-done(((f32[8192,64]{0,1:T(8,128)}), f32[8192,64]{0,1:T(8,128)}) %all-reduce.22.cloned.1.call-update) | async-done | bytes 2097168 | tf_op jit(solution)/shard_map/psum | solution.py:65
  327.3 7.6 fusion.22
  335.2 20.4 %all-reduce.38.cloned.1.call-done = (f32[64,64]{1,0:T(8,128)}, f32[64,64]{1,0:T(8,128)}, f32[64,64]{1,0:T(8,128)}, f32[64,64]{1,0:T(8,128)}) async-done(((f32[64,64]{1,0:T(8,128)}, f32[64,64]{1,0:T(8,128)}, f32[64,64]{1,0:T(8,128)}, f32[64,64]{1,0:T(8,128)}), (f32[64,64]{1,0:T(8,128)}, f32[64,64]{1,0:T(8,128)}, f32[64,64]{1,0:T(8,128)}, f32[64,64]{1,0:T(8,128)})) %all-reduce.38.cloned.1.call-update) | async-done | bytes 65552 | tf_op jit(solution)/shard_map/psum | solution.py:50
  378.6 14.8 %all-reduce.24.cloned.1.call-done = f32[768,64]{0,1:T(8,128)} async-done(((f32[768,64]{0,1:T(8,128)}), f32[768,64]{0,1:T(8,128)}) %all-reduce.24.cloned.1.call-update) | async-done | bytes 196624 | tf_op jit(solution)/shard_map/psum | solution.py:50
  396.3 8.4 fusion.72
  404.8 8.6 fusion.4
  415.8 27.8 %convolution_bitcast_fusion.4 = f32[4096,64]{0,1:T(8,128)S(1)} fusion(bf16[4096,8192]{1,0:T(8,128)(2,1)} %param.11, f32[8192,64]{0,1:T(8,128)S(1)} %convolution_add_fusion.2), kind=kOutput, calls=%fused_computation.17 | convolution fusion | flops 4295491584 | bytes 70254592 | tf_op jit(solution)/shard_map/dot_general | solution.py:60
  443.6 42.1 %all-reduce.40 = bf16[4096,64]{0,1:T(8,128)(2,1)} all-reduce(f32[4096,64]{0,1:T(8,128)S(1)} %convolution_bitcast_fusion.4), channel_id=1, replica_groups=mesh['samples'=4,'features'=4,'rhs'=2] {'features'}, use_global_device_ids=true, to_apply=%region_12.0 | all-reduce | flops 262144 | bytes 1572864 | tf_op jit(solution)/shard_map/psum | solution.py:61
  485.8 25.9 %convolution_bitcast_fusion.1 = f32[8192,64]{0,1:T(8,128)} fusion(bf16[4096,8192]{1,0:T(8,128)(2,1)} %param.11, bf16[4096,64]{0,1:T(8,128)(2,1)} %all-reduce.40), kind=kOutput, calls=%fused_computation.5 | convolution fusion | flops 4294967296 | bytes 69730304 | tf_op jit(solution)/shard_map/dot_general | solution.py:62
  511.8 20.9 %all-reduce.26.cloned.1.call-done = f32[8192,64]{0,1:T(8,128)} async-done(((f32[8192,64]{0,1:T(8,128)}), f32[8192,64]{0,1:T(8,128)}) %all-reduce.26.cloned.1.call-update) | async-done | bytes 2097168 | tf_op jit(solution)/shard_map/psum | solution.py:65
  537.2 69.3 %all-reduce.28.cloned.1.call-done = f32[8192,64]{0,1:T(8,128)} async-done(((f32[8192,64]{0,1:T(8,128)}), f32[8192,64]{0,1:T(8,128)}) %all-reduce.28.cloned.1.call-update) | async-done | bytes 2097168 | tf_op jit(solution)/shard_map/psum | solution.py:65
  623.6 7.6 fusion.23
  631.4 20.3 %all-reduce.36.cloned.1.call-done = (f32[64,64]{1,0:T(8,128)}, f32[64,64]{1,0:T(8,128)}, f32[64,64]{1,0:T(8,128)}, f32[64,64]{1,0:T(8,128)}) async-done(((f32[64,64]{1,0:T(8,128)}, f32[64,64]{1,0:T(8,128)}, f32[64,64]{1,0:T(8,128)}, f32[64,64]{1,0:T(8,128)}), (f32[64,64]{1,0:T(8,128)}, f32[64,64]{1,0:T(8,128)}, f32[64,64]{1,0:T(8,128)}, f32[64,64]{1,0:T(8,128)})) %all-reduce.36.cloned.1.call-update) | async-done | bytes 65552 | tf_op jit(solution)/shard_map/psum | solution.py:50
  674.8 14.8 %all-reduce.30.cloned.1.call-done = f32[768,64]{0,1:T(8,128)} async-done(((f32[768,64]{0,1:T(8,128)}), f32[768,64]{0,1:T(8,128)}) %all-reduce.30.cloned.1.call-update) | async-done | bytes 196624 | tf_op jit(solution)/shard_map/psum | solution.py:50
  692.6 8.4 fusion.79
  701.1 8.6 fusion.5
  711.9 27.1 %convolution_bitcast_fusion.3 = f32[4096,64]{0,1:T(8,128)S(1)} fusion(bf16[4096,8192]{1,0:T(8,128)(2,1)} %param.11, f32[8192,64]{0,1:T(8,128)S(1)} %convolution_add_fusion), kind=kOutput, calls=%fused_computation.16 | convolution fusion | flops 4295491584 | bytes 70254592 | tf_op jit(solution)/shard_map/dot_general | solution.py:60
  739.0 42.1 %all-reduce.41 = bf16[4096,64]{0,1:T(8,128)(2,1)} all-reduce(f32[4096,64]{0,1:T(8,128)S(1)} %convolution_bitcast_fusion.3), channel_id=1, replica_groups=mesh['samples'=4,'features'=4,'rhs'=2] {'features'}, use_global_device_ids=true, to_apply=%region_20.0 | all-reduce | flops 262144 | bytes 1572864 | tf_op jit(solution)/shard_map/psum | solution.py:61
  781.1 25.9 %convolution_bitcast_fusion = f32[8192,64]{0,1:T(8,128)} fusion(bf16[4096,8192]{1,0:T(8,128)(2,1)} %param.11, bf16[4096,64]{0,1:T(8,128)(2,1)} %all-reduce.41), kind=kOutput, calls=%fused_computation | convolution fusion | flops 4294967296 | bytes 69730304 | tf_op jit(solution)/shard_map/dot_general | solution.py:62
  807.6 20.5 %all-reduce.32.cloned.1.call-done = f32[8192,64]{0,1:T(8,128)} async-done(((f32[8192,64]{0,1:T(8,128)}), f32[8192,64]{0,1:T(8,128)}) %all-reduce.32.cloned.1.call-update) | async-done | bytes 2097168 | tf_op jit(solution)/shard_map/psum | solution.py:65
  838.3 63.6 %all-reduce.34.cloned.1.call-done = f32[8192,64]{0,1:T(8,128)} async-done(((f32[8192,64]{0,1:T(8,128)}), f32[8192,64]{0,1:T(8,128)}) %all-reduce.34.cloned.1.call-update) | async-done | bytes 2097168 | tf_op jit(solution)/shard_map/psum | solution.py:65
  905.4 20.0 %all-reduce = (f32[64,64]{1,0:T(8,128)S(1)}, f32[64,64]{1,0:T(8,128)S(1)}) all-reduce(f32[64,64]{1,0:T(8,128)S(1)} %fusion.19, f32[64,64]{1,0:T(8,128)S(1)} %fusion.83), channel_id=1, replica_groups=mesh['samples'=4,'features'=4,'rhs'=2] {'features'}, use_global_device_ids=true, to_apply=%region_23.28 | all-reduce | flops 8192 | bytes 65536 | tf_op jit(solution)/shard_map/psum | solution.py:50
  (158 shorter events, 144.4 us)
Async XLA Ops:
  7.2 15.7 %all-gather.3.cloned.1.call-start = ((), (), s32[]{:S(2)}) async-start(), calls=%async_computation | async-start | bytes 3145728 | tf_op jit(solution)/shard_map/all_gather | solution.py:45
  7.9 42.4 %all-gather.5.cloned.1.call-start = ((), (), s32[]{:S(2)}) async-start(), calls=%async_computation.1 | async-start | bytes 18874368 | tf_op jit(solution)/shard_map/all_gather | solution.py:47
  8.7 89.1 %all-reduce.18.cloned.1.call-start = ((), (), s32[]{:S(2)}) async-start(), calls=%async_computation.2 | async-start | bytes 393216 | tf_op jit(solution)/shard_map/psum | solution.py:50
  22.8 27.4 %copy-start.1 = (f32[8192,64]{0,1:T(8,128)S(1)}, f32[8192,64]{0,1:T(8,128)}, u32[]{:S(2)}) copy-start(f32[8192,64]{0,1:T(8,128)} %all-gather.3.cloned.1.call-done) | copy-start | bytes 6291460
  50.3 8.2 copy-start
  61.5 175.5 %all-reduce.20.cloned.1.call-start = ((), (), s32[]{:S(2)}) async-start(), calls=%async_computation.3 | async-start | bytes 4194304 | tf_op jit(solution)/shard_map/psum | solution.py:65
  98.7 8.5 copy-start.19
  216.2 94.5 %all-reduce.22.cloned.1.call-start = ((), (), s32[]{:S(2)}) async-start(), calls=%async_computation.4 | async-start | bytes 4194304 | tf_op jit(solution)/shard_map/psum | solution.py:65
  237.0 118.5 %all-reduce.38.cloned.1.call-start = ((), (), s32[]{:S(2)}) async-start(), calls=%async_computation.12 | async-start | bytes 262144 | tf_op jit(solution)/shard_map/psum | solution.py:50
  313.1 2.4 copy-start.4
  315.5 2.4 copy-start.2
  320.4 72.9 %all-reduce.24.cloned.1.call-start = ((), (), s32[]{:S(2)}) async-start(), calls=%async_computation.5 | async-start | bytes 393216 | tf_op jit(solution)/shard_map/psum | solution.py:50
  334.9 197.8 %all-reduce.26.cloned.1.call-start = ((), (), s32[]{:S(2)}) async-start(), calls=%async_computation.6 | async-start | bytes 4194304 | tf_op jit(solution)/shard_map/psum | solution.py:65
  376.3 19.6 %copy-start.24 = (f32[64,64]{1,0:T(8,128)S(1)}, f32[64,64]{1,0:T(8,128)}, u32[]{:S(2)}) copy-start(f32[64,64]{1,0:T(8,128)} %get-tuple-element.14) | copy-start | bytes 49156
  376.3 19.6 %copy-start.25 = (f32[64,64]{1,0:T(8,128)S(1)}, f32[64,64]{1,0:T(8,128)}, u32[]{:S(2)}) copy-start(f32[64,64]{1,0:T(8,128)} %get-tuple-element.15) | copy-start | bytes 49156
  378.4 26.4 %copy-start.7 = (f32[8192,64]{0,1:T(8,128)}, f32[8192,64]{0,1:T(8,128)S(1)}, u32[]{:S(2)}) copy-start(f32[8192,64]{0,1:T(8,128)S(1)} %convolution_subtract_fusion.1) | copy-start | bytes 6291460
  404.8 8.7 copy-start.13
  415.8 117.4 %copy-start.5 = (f32[8192,64]{0,1:T(8,128)}, f32[8192,64]{0,1:T(8,128)S(1)}, u32[]{:S(2)}) copy-start(f32[8192,64]{0,1:T(8,128)S(1)} %convolution_add_fusion.2) | copy-start | bytes 6291460
  511.7 94.8 %all-reduce.28.cloned.1.call-start = ((), (), s32[]{:S(2)}) async-start(), calls=%async_computation.7 | async-start | bytes 4194304 | tf_op jit(solution)/shard_map/psum | solution.py:65
  532.8 119.0 %all-reduce.36.cloned.1.call-start = ((), (), s32[]{:S(2)}) async-start(), calls=%async_computation.11 | async-start | bytes 262144 | tf_op jit(solution)/shard_map/psum | solution.py:50
  606.5 2.9 copy-start.8
  616.7 73.0 %all-reduce.30.cloned.1.call-start = ((), (), s32[]{:S(2)}) async-start(), calls=%async_computation.8 | async-start | bytes 393216 | tf_op jit(solution)/shard_map/psum | solution.py:50
  631.2 196.9 %all-reduce.32.cloned.1.call-start = ((), (), s32[]{:S(2)}) async-start(), calls=%async_computation.9 | async-start | bytes 4194304 | tf_op jit(solution)/shard_map/psum | solution.py:65
  672.5 19.7 %copy-start.22 = (f32[64,64]{1,0:T(8,128)S(1)}, f32[64,64]{1,0:T(8,128)}, u32[]{:S(2)}) copy-start(f32[64,64]{1,0:T(8,128)} %get-tuple-element.10) | copy-start | bytes 49156
  672.5 19.7 %copy-start.23 = (f32[64,64]{1,0:T(8,128)S(1)}, f32[64,64]{1,0:T(8,128)}, u32[]{:S(2)}) copy-start(f32[64,64]{1,0:T(8,128)} %get-tuple-element.11) | copy-start | bytes 49156
  674.6 26.5 %copy-start.10 = (f32[8192,64]{0,1:T(8,128)}, f32[8192,64]{0,1:T(8,128)S(1)}, u32[]{:S(2)}) copy-start(f32[8192,64]{0,1:T(8,128)S(1)} %convolution_subtract_fusion) | copy-start | bytes 6291460
  701.1 8.6 copy-start.14
  807.1 21.1 %copy-start.21 = (f32[64,64]{1,0:T(8,128)S(1)}, f32[64,64]{1,0:T(8,128)}, u32[]{:S(2)}) copy-start(f32[64,64]{1,0:T(8,128)} %copy-done.20) | copy-start | bytes 49156
  807.1 94.8 %all-reduce.34.cloned.1.call-start = ((), (), s32[]{:S(2)}) async-start(), calls=%async_computation.10 | async-start | bytes 4194304 | tf_op jit(solution)/shard_map/psum | solution.py:65
  828.2 5.0 copy-start.15
  833.1 3.3 copy-start.11
  941.9 4.1 copy-start.18
  (10 other events, 19.8 us)
Sparse Core Ops, SparseCore 0:
  9.5 13.2 all-gather.2
  24.4 25.8 all-gather.4
  61.6 36.1 all-reduce.17
  216.3 20.6 all-reduce.19
  240.0 70.6 all-reduce.21
  320.6 34.9 all-reduce.37
  358.4 34.8 all-reduce.23
  511.9 20.8 all-reduce.25
  535.8 70.6 all-reduce.27
  616.8 34.9 all-reduce.35
  654.7 34.9 all-reduce.29
  807.2 20.8 all-reduce.31
  831.2 70.6 all-reduce.33
